TPU v7x, 512 devices: a whole 4x4x16 slice. The times are simulated.
512 devices in a mesh: blk: 32 (over y, z_lo, core), replica: 16 (over z_hi, x).
Axes of the slice: x: 4, y: 4, z: 16 (z_hi: 4, z_lo: 4; z = z_hi * 4 + z_lo), core: 2. Of those that a mesh axis runs over, the one named last changes fastest.
Arguments:
- tokens: bfloat16 [640, 4096], P('blk', 'replica'), may hold values from -6 to 6
- cotangent: bfloat16 [640, 4096], P('blk', 'replica'), may hold values from -6 to 6
- gate_weight: bfloat16 [4096, 28672], P('replica', 'blk'), may hold values from -36 to 36, as said below
- up_weight: bfloat16 [4096, 28672], P('replica', 'blk'), may hold values from -36 to 36, as said below
- down_weight: bfloat16 [28672, 4096], P('blk', 'replica'), may hold values from -72 to 72, as said below
- gate_gain: float32 [28672], P('blk'), may hold values from 0.25 to 1.75
- up_gain: float32 [28672], P('blk'), may hold values from 0.25 to 1.75
- down_gain: float32 [4096], P('replica'), may hold values from 0.25 to 1.75
Outputs:
- grad_tokens: float32 [640, 4096], P('blk', 'replica')
- grad_gate: float32 [4096, 28672], P('replica', 'blk')
- grad_up: float32 [4096, 28672], P('replica', 'blk')
- grad_down: float32 [28672, 4096], P('blk', 'replica')
- grad_gate_gain: float32 [28672], P('blk')
- grad_up_gain: float32 [28672], P('blk')
- grad_down_gain: float32 [4096], P('replica')
Inputs may be any that keep to these rules, and one draw needn't show every extreme that they name: `gate_weight`: real-valued raw weights. `up_weight`: real-valued raw weights. `down_weight`: real-valued raw weights.
All inputs are finite; a program needn't handle non-finite values.
Results may differ from a plain program's by a relative error of at most 0.033.
Values may be sent and summed in bfloat16 or wider, within the bound.
No kernel may reach another device: no remote copies, remote signals or barrier semaphores. Data moves between devices by JAX's collectives and lax.ppermute only.
A program may use at most 64 MiB of HBM per device.

v0:
```python
import jax
import jax.numpy as jnp
from jax import lax
from jax.sharding import PartitionSpec as P

epsilon = 0.0001
branch_scale = 0.5


def sent_to_all(x, axis):
    copies = jnp.broadcast_to(x, (lax.axis_size(axis), *x.shape))
    return lax.all_to_all(copies, axis, split_axis=0, concat_axis=0, tiled=True)


def of_everyone(x, axis):
    return sent_to_all(x, axis).sum(axis=0)


def in_one(arrays, axis):
    ends = [0]
    for a in arrays:
        ends.append(ends[-1] + a.size)
    subtotal = of_everyone(jnp.concatenate([a.ravel() for a in arrays]), axis)
    return tuple((subtotal[b:e].reshape(a.shape) for a, b, e in zip(arrays, ends, ends[1:])))


def sent_together(arrays, axis, dim, along):
    both = jnp.concatenate(arrays, axis=along)
    result, at, done = (lax.all_gather(both, axis, axis=dim, tiled=True), 0, [])
    for a in arrays:
        done.append(lax.slice_in_dim(result, at, at + a.shape[along], axis=along))
        at += a.shape[along]
    return tuple(done)


def split_up(x, dim, devices):
    before, after = (x.shape[:dim], x.shape[dim + 1 :])
    return jnp.moveaxis(x.reshape(*before, devices, -1, *after), dim, 0)


def sum_at_owner(x, axis, dim):
    parts = split_up(x, dim, lax.axis_size(axis))
    arrived = lax.all_to_all(parts, axis, split_axis=0, concat_axis=0, tiled=True)
    return arrived.astype(jnp.float32).sum(axis=0)


def contract_first(left, right):
    return lax.dot_general(
        left, right, (((0,), (0,)), ((), ())), preferred_element_type=jnp.float32
    )


def contract_last(left, right):
    return lax.dot_general(
        left, right, (((1,), (1,)), ((), ())), preferred_element_type=jnp.float32
    )


def weight_grad(grad_hat, gain, cent, scale, summed, crossed, count):
    grad = scale * (gain * grad_hat - gain * summed / count) - scale * scale * scale * cent * (
        gain * crossed
    )
    return (grad, scale * crossed)


def gating(gate, up, dhidden):
    act = jax.nn.silu(gate)
    hidden = (act * up).astype(jnp.bfloat16)
    sig = jax.nn.sigmoid(gate)
    d_gate = (dhidden * up * sig * (1.0 + gate * (1.0 - sig))).astype(jnp.bfloat16)
    d_up = (dhidden * act).astype(jnp.bfloat16)
    return (d_gate, d_up, hidden)


def local(tokens, cotangent, gate_weight, up_weight, down_weight, gate_gain, up_gain, down_gain):
    width_all = gate_weight.shape[0] * lax.axis_size("replica")
    hidden_all = down_weight.shape[0] * lax.axis_size("blk")
    gate_raw = gate_weight.astype(jnp.float32)
    up_raw = up_weight.astype(jnp.float32)
    down_raw = down_weight.astype(jnp.float32)
    gate_sum, gate_power, up_sum, up_power = in_one(
        (
            jnp.sum(gate_raw, axis=0),
            jnp.sum(gate_raw * gate_raw, axis=0),
            jnp.sum(up_raw, axis=0),
            jnp.sum(up_raw * up_raw, axis=0),
        ),
        "replica",
    )
    gate_mean = gate_sum / width_all
    up_mean = up_sum / width_all
    gate_cent = gate_raw - gate_mean
    up_cent = up_raw - up_mean
    gate_square = gate_power - gate_sum * gate_mean
    up_square = up_power - up_sum * up_mean
    down_sum, down_power = in_one(
        (jnp.sum(down_raw, axis=0), jnp.sum(down_raw * down_raw, axis=0)), "blk"
    )
    down_mean = down_sum / hidden_all
    down_cent = down_raw - down_mean
    down_square = down_power - down_sum * down_mean
    gate_scale = lax.rsqrt(gate_square + epsilon)
    up_scale = lax.rsqrt(up_square + epsilon)
    down_scale = lax.rsqrt(down_square + epsilon)
    gate_hat = (gate_gain * gate_cent * gate_scale).astype(jnp.bfloat16)
    up_hat = (up_gain * up_cent * up_scale).astype(jnp.bfloat16)
    down_hat = (down_gain * down_cent * down_scale).astype(jnp.bfloat16)
    scaled = (branch_scale * cotangent.astype(jnp.float32)).astype(jnp.bfloat16)
    whole_tokens, whole_scaled = sent_together((tokens, scaled), "blk", 0, 1)
    gate_part = jnp.dot(whole_tokens, gate_hat, preferred_element_type=jnp.float32).astype(
        jnp.bfloat16
    )
    up_part = jnp.dot(whole_tokens, up_hat, preferred_element_type=jnp.float32).astype(jnp.bfloat16)
    down_part = contract_last(whole_scaled, down_hat).astype(jnp.bfloat16)
    gate, up, dhidden = (
        lax.psum(gate_part, "replica").astype(jnp.float32),
        lax.psum(up_part, "replica").astype(jnp.float32),
        lax.psum(down_part, "replica").astype(jnp.float32),
    )
    d_gate, d_up, hidden = gating(gate, up, dhidden)
    share = sum_at_owner(
        (contract_last(d_gate, gate_hat) + contract_last(d_up, up_hat)).astype(jnp.bfloat16),
        "blk",
        0,
    )
    grad_tokens = cotangent.astype(jnp.float32) + share
    p_gate = contract_first(whole_tokens, d_gate)
    p_up = contract_first(whole_tokens, d_up)
    p_down = contract_first(hidden, whole_scaled)
    gate_psum, gate_pcross, up_psum, up_pcross = in_one(
        (
            jnp.sum(p_gate, axis=0),
            jnp.sum(p_gate * gate_cent, axis=0),
            jnp.sum(p_up, axis=0),
            jnp.sum(p_up * up_cent, axis=0),
        ),
        "replica",
    )
    down_psum, down_pcross = in_one(
        (jnp.sum(p_down, axis=0), jnp.sum(p_down * down_cent, axis=0)), "blk"
    )
    grad_gate, grad_gate_gain = weight_grad(
        p_gate, gate_gain, gate_cent, gate_scale, gate_psum, gate_pcross, width_all
    )
    grad_up, grad_up_gain = weight_grad(
        p_up, up_gain, up_cent, up_scale, up_psum, up_pcross, width_all
    )
    grad_down, grad_down_gain = weight_grad(
        p_down, down_gain, down_cent, down_scale, down_psum, down_pcross, hidden_all
    )
    return (
        grad_tokens,
        grad_gate,
        grad_up,
        grad_down,
        grad_gate_gain,
        grad_up_gain,
        grad_down_gain,
    )


def solution(mesh):
    return jax.shard_map(
        local,
        mesh=mesh,
        in_specs=(
            P("blk", "replica"),
            P("blk", "replica"),
            P("replica", "blk"),
            P("replica", "blk"),
            P("blk", "replica"),
            P("blk"),
            P("blk"),
            P("replica"),
        ),
        out_specs=(
            P("blk", "replica"),
            P("replica", "blk"),
            P("replica", "blk"),
            P("blk", "replica"),
            P("blk"),
            P("blk"),
            P("replica"),
        ),
        check_vma=False,
    )
```

profile of v0, /device:TPU:1, one launch (start us, length us, event | category | flops | bytes accessed | tf_op | source)
XLA Modules:
  0.0 533.1 jit_solution(5313933197506070054)
XLA Ops:
  9.1 10.3 %all-to-all-start = ((f32[32,1,512]{2,1,0:T(1,128)}), f32[32,1,512]{2,1,0:T(1,128)S(1)}, u32[]{:S(2)}, u32[]{:S(2)}) async-start(f32[32,1,512]{2,1,0:T(1,128)} %broadcast_in_dim.8), calls=%async_computation | async-start | bytes 131072 | tf_op jit(solution)/shard_map/all_to_all | solution.py:12
  19.4 1.4 convert_reduce_fusion
  20.9 6.4 %all-to-all-done = f32[32,1,512]{2,1,0:T(1,128)S(1)} async-done(((f32[32,1,512]{2,1,0:T(1,128)}), f32[32,1,512]{2,1,0:T(1,128)S(1)}, u32[]{:S(2)}, u32[]{:S(2)}) %all-to-all-start) | async-done | bytes 65568 | tf_op jit(solution)/shard_map/all_to_all | solution.py:12
  28.1 14.4 %all-to-all-start.1 = ((f32[16,1,3584]{2,1,0:T(1,128)}), f32[16,1,3584]{2,1,0:T(1,128)S(1)}, u32[]{:S(2)}, u32[]{:S(2)}) async-start(f32[16,1,3584]{2,1,0:T(1,128)} %broadcast_in_dim.9), calls=%async_computation.1 | async-start | bytes 458752 | tf_op jit(solution)/shard_map/all_to_all | solution.py:12
  42.6 46.4 %all-gather = bf16[32,20,512]{2,1,0:T(8,128)(2,1)S(1)} all-gather(bf16[1,20,512]{2,1,0:T(8,128)(2,1)S(1)} %maximum_bitcast_fusion), channel_id=1, replica_groups=mesh['blk'=32,'replica'=16] {'blk'}, dimensions={0}, use_global_device_ids=true | all-gather | bytes 675840 | tf_op jit(solution)/shard_map/all_gather | solution.py:29
  89.9 1.6 convolution_convert_fusion.2
  92.3 1.6 convolution_convert_fusion
  93.9 1.6 convolution_convert_fusion.1
  95.5 358.5 %all-reduce.3.cloned.1.call-done = (bf16[640,896]{1,0:T(8,128)(2,1)}, bf16[640,896]{1,0:T(8,128)(2,1)}, bf16[640,896]{1,0:T(8,128)(2,1)}) async-done(((bf16[640,896]{1,0:T(8,128)(2,1)}, bf16[640,896]{1,0:T(8,128)(2,1)}, bf16[640,896]{1,0:T(8,128)(2,1)}), (bf16[640,896]{1,0:T(8,128)(2,1)}, bf16[640,896]{1,0:T(8,128)(2,1)}, bf16[640,896]{1,0:T(8,128)(2,1)})) %all-reduce.3.cloned.1.call-update) | async-done | bytes 3440656 | tf_op jit(solution)/shard_map/psum | solution.py:117
  454.1 3.7 fusion.64
  457.7 2.3 fusion
  460.7 6.7 %all-to-all-start.4 = ((f32[32,1,512]{2,1,0:T(1,128)}), f32[32,1,512]{2,1,0:T(1,128)S(1)}, u32[]{:S(2)}, u32[]{:S(2)}) async-start(f32[32,1,512]{2,1,0:T(1,128)} %broadcast_in_dim.11), calls=%async_computation.4 | async-start | bytes 131072 | tf_op jit(solution)/shard_map/all_to_all | solution.py:12
  467.4 1.7 fusion.66
  469.2 1.5 fusion.65
  470.7 4.5 all-to-all-done.4
  476.0 10.2 %all-to-all-start.3 = ((f32[16,1,3584]{2,1,0:T(1,128)}), f32[16,1,3584]{2,1,0:T(1,128)}, u32[]{:S(2)}, u32[]{:S(2)}) async-start(f32[16,1,3584]{2,1,0:T(1,128)} %broadcast_in_dim.10), calls=%async_computation.3 | async-start | bytes 458752 | tf_op jit(solution)/shard_map/all_to_all | solution.py:12
  486.2 1.8 fusion.45
  488.0 1.3 fusion.18
  489.3 1.8 reshape.51
  491.2 11.7 %all-to-all-done.3 = f32[16,1,3584]{2,1,0:T(1,128)} async-done(((f32[16,1,3584]{2,1,0:T(1,128)}), f32[16,1,3584]{2,1,0:T(1,128)}, u32[]{:S(2)}, u32[]{:S(2)}) %all-to-all-start.3) | async-done | bytes 229408 | tf_op jit(solution)/shard_map/all_to_all | solution.py:12
  502.9 8.6 %all-to-all-start.2 = ((bf16[32,20,256]{2,1,0:T(8,128)(2,1)}), bf16[32,20,256]{2,1,0:T(8,128)(2,1)S(1)}, u32[]{:S(2)}, u32[]{:S(2)}) async-start(bf16[32,20,256]{2,1,0:T(8,128)(2,1)} %reshape.51), calls=%async_computation.2 | async-start | bytes 786432 | tf_op jit(solution)/shard_map/all_to_all | solution.py:43
  512.1 2.4 fusion.35
  516.2 2.3 fusion.25
  519.7 5.8 %all-to-all-done.2 = bf16[32,20,256]{2,1,0:T(8,128)(2,1)S(1)} async-done(((bf16[32,20,256]{2,1,0:T(8,128)(2,1)}), bf16[32,20,256]{2,1,0:T(8,128)(2,1)S(1)}, u32[]{:S(2)}, u32[]{:S(2)}) %all-to-all-start.2) | async-done | bytes 327712 | tf_op jit(solution)/shard_map/all_to_all | solution.py:43
  (76 shorter events, 10.2 us)
Async XLA Ops:
  7.2 13.7 %copy-start.9 = (bf16[20,256]{1,0:T(8,128)(2,1)S(1)}, bf16[20,256]{1,0:T(8,128)(2,1)}, u32[]{:S(2)}) copy-start(bf16[20,256]{1,0:T(8,128)(2,1)} %param.9) | copy-start | bytes 30724
  7.2 35.4 %copy-start.17 = (bf16[20,256]{1,0:T(8,128)(2,1)S(1)}, bf16[20,256]{1,0:T(8,128)(2,1)}, u32[]{:S(2)}) copy-start(bf16[20,256]{1,0:T(8,128)(2,1)} %param.8) | copy-start | bytes 30724
  9.1 18.2 %all-to-all-start = ((f32[32,1,512]{2,1,0:T(1,128)}), f32[32,1,512]{2,1,0:T(1,128)S(1)}, u32[]{:S(2)}, u32[]{:S(2)}) async-start(f32[32,1,512]{2,1,0:T(1,128)} %broadcast_in_dim.8), calls=%async_computation | async-start | bytes 131072 | tf_op jit(solution)/shard_map/all_to_all | solution.py:12
  28.1 63.4 %all-to-all-start.1 = ((f32[16,1,3584]{2,1,0:T(1,128)}), f32[16,1,3584]{2,1,0:T(1,128)S(1)}, u32[]{:S(2)}, u32[]{:S(2)}) async-start(f32[16,1,3584]{2,1,0:T(1,128)} %broadcast_in_dim.9), calls=%async_computation.1 | async-start | bytes 458752 | tf_op jit(solution)/shard_map/all_to_all | solution.py:12
  42.5 411.5 %all-reduce.3.cloned.1.call-start = ((), (), s32[]{:S(2)}) async-start(), calls=%async_computation.5 | async-start | bytes 6881280 | tf_op jit(solution)/shard_map/psum | solution.py:117
  42.6 47.3 %copy-start = (bf16[896,256]{1,0:T(8,128)(2,1)S(1)}, bf16[896,256]{1,0:T(8,128)(2,1)}, u32[]{:S(2)}) copy-start(bf16[896,256]{1,0:T(8,128)(2,1)} %param.12) | copy-start | bytes 1376260
  42.6 47.3 %copy-start.20 = (f32[256]{0:T(256)S(1)}, f32[256]{0:T(256)}, u32[]{:S(2)}) copy-start(f32[256]{0:T(256)} %param.15) | copy-start | bytes 3076
  89.1 364.9 %copy-start.7 = (bf16[640,512]{1,0:T(8,128)(2,1)}, bf16[640,512]{1,0:T(8,128)(2,1)S(1)}, u32[]{:S(2)}) copy-start(bf16[640,512]{1,0:T(8,128)(2,1)S(1)} %reshape.53) | copy-start | bytes 1966084
  89.9 364.2 %copy-start.23 = (f32[256]{0:T(256)}, f32[256]{0:T(256)S(1)}, u32[]{:S(2)}) copy-start(f32[256]{0:T(256)S(1)} %get-tuple-element.46) | copy-start | bytes 3076
  89.9 2.4 copy-start.1
  92.3 375.1 %copy-start.12 = (f32[896]{0:T(1024)}, f32[896]{0:T(1024)S(1)}, u32[]{:S(2)}) copy-start(f32[896]{0:T(1024)S(1)} %get-tuple-element.42) | copy-start | bytes 10756
  92.3 376.9 %copy-start.15 = (f32[896]{0:T(1024)}, f32[896]{0:T(1024)S(1)}, u32[]{:S(2)}) copy-start(f32[896]{0:T(1024)S(1)} %get-tuple-element.39) | copy-start | bytes 10756
  454.0 3.7 copy-start.4
  454.1 3.7 copy-start.5
  454.1 3.7 copy-start.6
  460.7 14.5 %all-to-all-start.4 = ((f32[32,1,512]{2,1,0:T(1,128)}), f32[32,1,512]{2,1,0:T(1,128)S(1)}, u32[]{:S(2)}, u32[]{:S(2)}) async-start(f32[32,1,512]{2,1,0:T(1,128)} %broadcast_in_dim.11), calls=%async_computation.4 | async-start | bytes 131072 | tf_op jit(solution)/shard_map/all_to_all | solution.py:12
  476.0 26.9 %all-to-all-start.3 = ((f32[16,1,3584]{2,1,0:T(1,128)}), f32[16,1,3584]{2,1,0:T(1,128)}, u32[]{:S(2)}, u32[]{:S(2)}) async-start(f32[16,1,3584]{2,1,0:T(1,128)} %broadcast_in_dim.10), calls=%async_computation.3 | async-start | bytes 458752 | tf_op jit(solution)/shard_map/all_to_all | solution.py:12
  489.3 22.2 %copy-start.19 = (f32[256]{0:T(256)S(1)}, f32[256]{0:T(256)}, u32[]{:S(2)}) copy-start(f32[256]{0:T(256)} %copy-done.18) | copy-start | bytes 3076
  489.3 22.2 %copy-start.21 = (f32[256]{0:T(256)S(1)}, f32[256]{0:T(256)}, u32[]{:S(2)}) copy-start(f32[256]{0:T(256)} %param.15) | copy-start | bytes 3076
  489.3 22.8 %copy-start.22 = (f32[256]{0:T(256)S(1)}, f32[256]{0:T(256)}, u32[]{:S(2)}) copy-start(f32[256]{0:T(256)} %get-tuple-element.22) | copy-start | bytes 3076
  489.3 22.8 %copy-start.24 = (f32[256]{0:T(256)S(1)}, f32[256]{0:T(256)}, u32[]{:S(2)}) copy-start(f32[256]{0:T(256)} %copy-done.23) | copy-start | bytes 3076
  502.9 22.7 %all-to-all-start.2 = ((bf16[32,20,256]{2,1,0:T(8,128)(2,1)}), bf16[32,20,256]{2,1,0:T(8,128)(2,1)S(1)}, u32[]{:S(2)}, u32[]{:S(2)}) async-start(bf16[32,20,256]{2,1,0:T(8,128)(2,1)} %reshape.51), calls=%async_computation.2 | async-start | bytes 786432 | tf_op jit(solution)/shard_map/all_to_all | solution.py:43
  512.1 4.1 copy-start.14
  512.1 4.1 copy-start.16
  (7 other events, 14.1 us)
Sparse Core Ops, SparseCore 0:
  95.6 358.3 all-reduce.2
where the time goes:
time: 534 us; the launch traced here: 533 us
  waiting for transfers between devices  387 us (72%)
  starting transfers between devices  50.3 us (9%)
  blocking collectives  46.4 us (9%)
  other arithmetic  15.3 us (3%)
  matrix products  14.7 us (3%)
  between operations  14.3 us (3%)
    psum x1, waiting for transfers between devices, local(): lax.psum(up_part, 'replica').astype(jnp.float32)  359 us
    all_gather x1, blocking collectives, sent_together(): result, at, done = (lax.all_gather(both, axis, axis=dim, tiled=True), 0, [])  46.4 us
    all_to_all x4, starting transfers between devices, sent_to_all(): return lax.all_to_all(copies, axis, split_axis=0, concat_axis=0, tiled=True)  41.6 us
    all_to_all x4, waiting for transfers between devices, sent_to_all(): return lax.all_to_all(copies, axis, split_axis=0, concat_axis=0, tiled=True)  22.6 us
  transfers between devices with their start and end apart: 6, of which 5 were waited for; matrix products, arithmetic and copies ran while one was open for 4% of the time, Pallas kernels for 0%

commit v1 on v0

--- a/solution.py
+++ b/solution.py
@@ -114,7 +114,7 @@
     down_part = contract_last(whole_scaled, down_hat).astype(jnp.bfloat16)
     gate, up, dhidden = (
         lax.psum(gate_part, "replica").astype(jnp.float32),
-        lax.psum(up_part, "replica").astype(jnp.float32),
+        jnp.sum(lax.all_gather(up_part, "replica"), axis=0).astype(jnp.float32),
         lax.psum(down_part, "replica").astype(jnp.float32),
     )
     d_gate, d_up, hidden = gating(gate, up, dhidden)

time: 534 us -> 852 us (1.60)
  waiting for transfers between devices: 387 us -> 683 us
  blocking collectives: 46.4 us -> 59.9 us
  other arithmetic: 15.3 us -> 24.6 us
    all_gather x0 -> x1, waiting for transfers between devices: none -> 400 us  [local(): lax.all_gather(up_part, 'replica')]
    psum x1, waiting for transfers between devices: 359 us -> 259 us  [local(): lax.psum(down_part, 'replica').astype(jnp.float32)]
    all_to_all x0 -> x1, blocking collectives: none -> 10.8 us  [sent_to_all(): return lax.all_to_all(copies, axis, split_axis=0, concat_axis=0, tiled=True)]
    reduce_sum x0 -> x1, other arithmetic: none -> 9.98 us  [local(): jnp.sum(lax.all_gather(up_part, 'replica'), axis=0).astype(jnp.float32)]
    all_to_all x4 -> x3, waiting for transfers between devices: 22.6 us -> 18.1 us  [sent_to_all(): return lax.all_to_all(copies, axis, split_axis=0, concat_axis=0, tiled=True)]
    all_to_all x4 -> x3, starting transfers between devices: 41.6 us -> 44 us  [sent_to_all(): return lax.all_to_all(copies, axis, split_axis=0, concat_axis=0, tiled=True)]
  transfers between devices with their start and end apart: 6 -> 6, of which waited for: 5 -> 5; matrix products, arithmetic and copies ran while one was open for 4% -> 3% of each run, Pallas kernels for 0% -> 0%
where the time goes in v1:
time: 852 us
  waiting for transfers between devices  683 us (80%)
  blocking collectives  59.9 us (7%)
  starting transfers between devices  53 us (6%)
  other arithmetic  24.6 us (3%)
  between operations  14.4 us (2%)
  matrix products  13.5 us (2%)
    all_gather x1, waiting for transfers between devices, local(): lax.all_gather(up_part, 'replica')  400 us
    psum x1, waiting for transfers between devices, local(): lax.psum(down_part, 'replica').astype(jnp.float32)  259 us
    all_gather x1, blocking collectives, sent_together(): result, at, done = (lax.all_gather(both, axis, axis=dim, tiled=True), 0, [])  49.1 us
    all_to_all x3, starting transfers between devices, sent_to_all(): return lax.all_to_all(copies, axis, split_axis=0, concat_axis=0, tiled=True)  44 us
    all_to_all x3, waiting for transfers between devices, sent_to_all(): return lax.all_to_all(copies, axis, split_axis=0, concat_axis=0, tiled=True)  18.1 us
  transfers between devices with their start and end apart: 6, of which 5 were waited for; matrix products, arithmetic and copies ran while one was open for 3% of the time, Pallas kernels for 0%

profile of v1, /device:TPU:1, one launch (start us, length us, event | category | flops | bytes accessed | tf_op | source)
XLA Modules:
  0.0 851.7 jit_solution(8520168053173441434)
XLA Ops:
  7.2 1.4 convert_reduce_fusion
  9.4 18.2 %all-to-all-start.1 = ((f32[16,1,3584]{2,1,0:T(1,128)}), f32[16,1,3584]{2,1,0:T(1,128)S(1)}, u32[]{:S(2)}, u32[]{:S(2)}) async-start(f32[16,1,3584]{2,1,0:T(1,128)} %broadcast_in_dim.9), calls=%async_computation.1 | async-start | bytes 458752 | tf_op jit(solution)/shard_map/all_to_all | solution.py:12
  27.8 49.1 %all-gather.1 = bf16[32,20,512]{2,1,0:T(8,128)(2,1)S(1)} all-gather(bf16[1,20,512]{2,1,0:T(8,128)(2,1)S(1)} %maximum_bitcast_fusion), channel_id=1, replica_groups=mesh['blk'=32,'replica'=16] {'blk'}, dimensions={0}, use_global_device_ids=true | all-gather | bytes 675840 | tf_op jit(solution)/shard_map/all_gather | solution.py:29
  77.9 1.6 convolution_convert_fusion.1
  79.7 10.8 %all_to_all.29 = f32[32,1,512]{2,1,0:T(1,128)S(1)} all-to-all(f32[32,1,512]{2,1,0:T(1,128)S(1)} %broadcast_in_dim.8), channel_id=1, replica_groups=mesh['blk'=32,'replica'=16] {'blk'}, dimensions={0} | all-to-all | bytes 131072 | tf_op jit(solution)/shard_map/all_to_all | solution.py:12
  91.2 1.6 convolution_convert_fusion.2
  92.8 1.6 convolution_convert_fusion
  94.4 399.8 %all-gather.4.cloned.1.call-done = bf16[10240,896]{1,0:T(8,128)(2,1)} async-done(((bf16[640,896]{1,0:T(8,128)(2,1)}), bf16[10240,896]{1,0:T(8,128)(2,1)}) %all-gather.4.cloned.1.call-update) | async-done | bytes 18350096 | tf_op jit(solution)/shard_map/all_gather | solution.py:117
  494.2 10.0 %reduce_sum.173 = bf16[640,896]{1,0:T(8,128)(2,1)S(1)} reduce(bf16[16,640,896]{2,1,0:T(8,128)(2,1)} %bitcast.7, bf16[]{:T(256)} %constant.21.clone.1), dimensions={0}, to_apply=%region_9.0 | reduce | flops 8601600 | bytes 19496962 | tf_op jit(solution)/shard_map/reduce_sum | solution.py:117
  504.2 259.2 %all-reduce.3.cloned.1.call-done = (bf16[640,896]{1,0:T(8,128)(2,1)}, bf16[640,896]{1,0:T(8,128)(2,1)}) async-done(((bf16[640,896]{1,0:T(8,128)(2,1)}, bf16[640,896]{1,0:T(8,128)(2,1)}), (bf16[640,896]{1,0:T(8,128)(2,1)}, bf16[640,896]{1,0:T(8,128)(2,1)})) %all-reduce.3.cloned.1.call-update) | async-done | bytes 2293776 | tf_op jit(solution)/shard_map/psum | solution.py:118
  763.4 3.3 fusion.64
  766.7 2.7 fusion
  770.0 14.2 %all-to-all-start.4 = ((f32[32,1,512]{2,1,0:T(1,128)}), f32[32,1,512]{2,1,0:T(1,128)S(1)}, u32[]{:S(2)}, u32[]{:S(2)}) async-start(f32[32,1,512]{2,1,0:T(1,128)} %broadcast_in_dim.11), calls=%async_computation.4 | async-start | bytes 131072 | tf_op jit(solution)/shard_map/all_to_all | solution.py:12
  784.3 2.1 fusion.66
  786.4 1.5 fusion.65
  787.9 4.2 all-to-all-done.4
  793.0 11.6 %all-to-all-start.3 = ((f32[16,1,3584]{2,1,0:T(1,128)}), f32[16,1,3584]{2,1,0:T(1,128)}, u32[]{:S(2)}, u32[]{:S(2)}) async-start(f32[16,1,3584]{2,1,0:T(1,128)} %broadcast_in_dim.10), calls=%async_computation.3 | async-start | bytes 458752 | tf_op jit(solution)/shard_map/all_to_all | solution.py:12
  804.6 1.3 fusion.45
  807.4 13.8 %all-to-all-done.3 = f32[16,1,3584]{2,1,0:T(1,128)} async-done(((f32[16,1,3584]{2,1,0:T(1,128)}), f32[16,1,3584]{2,1,0:T(1,128)}, u32[]{:S(2)}, u32[]{:S(2)}) %all-to-all-start.3) | async-done | bytes 229408 | tf_op jit(solution)/shard_map/all_to_all | solution.py:12
  821.3 8.9 %all-to-all-start.2 = ((bf16[32,20,256]{2,1,0:T(8,128)(2,1)}), bf16[32,20,256]{2,1,0:T(8,128)(2,1)S(1)}, u32[]{:S(2)}, u32[]{:S(2)}) async-start(bf16[32,20,256]{2,1,0:T(8,128)(2,1)} %reshape.51), calls=%async_computation.2 | async-start | bytes 786432 | tf_op jit(solution)/shard_map/all_to_all | solution.py:43
  830.8 2.4 fusion.35
  834.9 2.3 fusion.25
  837.2 1.2 fusion.30
  838.4 5.8 all-to-all-done.2
  (79 shorter events, 8.7 us)
Async XLA Ops:
  7.2 20.5 %copy-start.9 = (bf16[20,256]{1,0:T(8,128)(2,1)S(1)}, bf16[20,256]{1,0:T(8,128)(2,1)}, u32[]{:S(2)}) copy-start(bf16[20,256]{1,0:T(8,128)(2,1)} %param.9) | copy-start | bytes 30724
  7.2 20.5 %copy-start.17 = (bf16[20,256]{1,0:T(8,128)(2,1)S(1)}, bf16[20,256]{1,0:T(8,128)(2,1)}, u32[]{:S(2)}) copy-start(bf16[20,256]{1,0:T(8,128)(2,1)} %param.8) | copy-start | bytes 30724
  9.4 67.6 %all-to-all-start.1 = ((f32[16,1,3584]{2,1,0:T(1,128)}), f32[16,1,3584]{2,1,0:T(1,128)S(1)}, u32[]{:S(2)}, u32[]{:S(2)}) async-start(f32[16,1,3584]{2,1,0:T(1,128)} %broadcast_in_dim.9), calls=%async_computation.1 | async-start | bytes 458752 | tf_op jit(solution)/shard_map/all_to_all | solution.py:12
  27.6 466.5 %all-gather.4.cloned.1.call-start = ((), (), s32[]{:S(2)}) async-start(), calls=%async_computation.5 | async-start | bytes 19496960 | tf_op jit(solution)/shard_map/all_gather | solution.py:117
  27.7 50.1 %copy-start.2 = (bf16[256,896]{1,0:T(8,128)(2,1)S(1)}, bf16[256,896]{1,0:T(8,128)(2,1)}, u32[]{:S(2)}) copy-start(bf16[256,896]{1,0:T(8,128)(2,1)} %param.11) | copy-start | bytes 1376260
  27.8 50.1 %copy-start.11 = (f32[896]{0:T(1024)S(1)}, f32[896]{0:T(1024)}, u32[]{:S(2)}) copy-start(f32[896]{0:T(1024)} %param.14) | copy-start | bytes 10756
  77.0 686.4 %copy-start.7 = (bf16[640,512]{1,0:T(8,128)(2,1)}, bf16[640,512]{1,0:T(8,128)(2,1)S(1)}, u32[]{:S(2)}) copy-start(bf16[640,512]{1,0:T(8,128)(2,1)S(1)} %reshape.54) | copy-start | bytes 1966084
  77.8 706.4 %copy-start.12 = (f32[896]{0:T(1024)}, f32[896]{0:T(1024)S(1)}, u32[]{:S(2)}) copy-start(f32[896]{0:T(1024)S(1)} %get-tuple-element.41) | copy-start | bytes 10756
  77.8 708.6 %copy-start.15 = (f32[896]{0:T(1024)}, f32[896]{0:T(1024)S(1)}, u32[]{:S(2)}) copy-start(f32[896]{0:T(1024)S(1)} %get-tuple-element.38) | copy-start | bytes 10756
  79.4 11.8 %copy-start.20 = (f32[256]{0:T(256)S(1)}, f32[256]{0:T(256)}, u32[]{:S(2)}) copy-start(f32[256]{0:T(256)} %param.15) | copy-start | bytes 3076
  79.4 683.9 %all-reduce.3.cloned.1.call-start = ((), (), s32[]{:S(2)}) async-start(), calls=%async_computation.6 | async-start | bytes 4587520 | tf_op jit(solution)/shard_map/psum | solution.py:118
  79.7 13.1 %copy-start.1 = (bf16[256,896]{1,0:T(8,128)(2,1)S(1)}, bf16[256,896]{1,0:T(8,128)(2,1)}, u32[]{:S(2)}) copy-start(bf16[256,896]{1,0:T(8,128)(2,1)} %param.10) | copy-start | bytes 1376260
  79.7 13.1 %copy-start.10 = (f32[896]{0:T(1024)S(1)}, f32[896]{0:T(1024)}, u32[]{:S(2)}) copy-start(f32[896]{0:T(1024)} %param.13) | copy-start | bytes 10756
  91.2 672.2 %copy-start.23 = (f32[256]{0:T(256)}, f32[256]{0:T(256)S(1)}, u32[]{:S(2)}) copy-start(f32[256]{0:T(256)S(1)} %get-tuple-element.45) | copy-start | bytes 3076
  763.4 3.3 copy-start.6
  770.0 22.1 %all-to-all-start.4 = ((f32[32,1,512]{2,1,0:T(1,128)}), f32[32,1,512]{2,1,0:T(1,128)S(1)}, u32[]{:S(2)}, u32[]{:S(2)}) async-start(f32[32,1,512]{2,1,0:T(1,128)} %broadcast_in_dim.11), calls=%async_computation.4 | async-start | bytes 131072 | tf_op jit(solution)/shard_map/all_to_all | solution.py:12
  793.0 28.3 %all-to-all-start.3 = ((f32[16,1,3584]{2,1,0:T(1,128)}), f32[16,1,3584]{2,1,0:T(1,128)}, u32[]{:S(2)}, u32[]{:S(2)}) async-start(f32[16,1,3584]{2,1,0:T(1,128)} %broadcast_in_dim.10), calls=%async_computation.3 | async-start | bytes 458752 | tf_op jit(solution)/shard_map/all_to_all | solution.py:12
  806.5 23.7 %copy-start.19 = (f32[256]{0:T(256)S(1)}, f32[256]{0:T(256)}, u32[]{:S(2)}) copy-start(f32[256]{0:T(256)} %copy-done.18) | copy-start | bytes 3076
  806.5 23.7 %copy-start.21 = (f32[256]{0:T(256)S(1)}, f32[256]{0:T(256)}, u32[]{:S(2)}) copy-start(f32[256]{0:T(256)} %param.15) | copy-start | bytes 3076
  806.6 24.2 %copy-start.22 = (f32[256]{0:T(256)S(1)}, f32[256]{0:T(256)}, u32[]{:S(2)}) copy-start(f32[256]{0:T(256)} %get-tuple-element.21) | copy-start | bytes 3076
  806.6 24.2 %copy-start.24 = (f32[256]{0:T(256)S(1)}, f32[256]{0:T(256)}, u32[]{:S(2)}) copy-start(f32[256]{0:T(256)} %copy-done.23) | copy-start | bytes 3076
  821.3 22.9 %all-to-all-start.2 = ((bf16[32,20,256]{2,1,0:T(8,128)(2,1)}), bf16[32,20,256]{2,1,0:T(8,128)(2,1)S(1)}, u32[]{:S(2)}, u32[]{:S(2)}) async-start(bf16[32,20,256]{2,1,0:T(8,128)(2,1)} %reshape.51), calls=%async_computation.2 | async-start | bytes 786432 | tf_op jit(solution)/shard_map/all_to_all | solution.py:43
  830.8 4.1 copy-start.14
  830.8 4.1 copy-start.16
  (7 other events, 15.1 us)
Sparse Core Ops, SparseCore 0:
  79.6 414.5 all-gather.3
  497.2 266.1 all-reduce.2
